TPU v7x, 32 devices: a whole 2x2x4 slice. The times are simulated.
32 devices in a mesh: pb: 4 (over z), freq: 4 (over y, core), ga: 2 (over x).
Axes of the slice: x: 2, y: 2, z: 4, core: 2. Of those that a mesh axis runs over, the one named last changes fastest.
Arguments:
- densities: bfloat16 [4, 2, 256, 4096], P('pb', None, ('freq', 'ga')), may hold values from -0.5 to 0.5
- screened: bfloat16 [4, 4, 2, 4096, 4096], P('pb', 'freq', None, 'ga'), may hold values from -0.09375 to 0.09375
- energies: float32 [16, 256], replicated, may hold values from -2.5 to 2.5
- occupied: int32 [16], replicated, may hold values from 64 to 192
- kmq: int32 [4], replicated, may hold values from 0 to 15
- offsets: int32 [4], replicated, may hold values from -16 to 15
- weights: float32 [4], replicated, may hold values from 0.5 to 2
Outputs:
- sigma: float32 [2, 1, 64], P(None, None, ('pb', 'freq'))
All inputs are finite; a program needn't handle non-finite values.
Results may differ from a plain program's by a relative error of at most 0.0003.
Values may be sent and summed in bfloat16 or wider, within the bound.
A program may use at most 64 MiB of HBM per device.

v0:
```python
import math
import jax
import jax.numpy as jnp
from jax import lax
from jax.sharding import PartitionSpec as P

NB = 256
NS = 1
OUT_DEV = 4
broadening = 0.15


def from_behind(block, axis, distance):
    devices = range(lax.axis_size(axis))
    route = [((i - distance) % len(devices), i) for i in devices]
    return lax.ppermute(block, axis, route)


def green_parts(level_row, filled, freq_shift, omegas):
    bands = jnp.arange(level_row.shape[0], dtype=jnp.int32)
    pole_sign = jnp.where(bands < filled, -1.0, 1.0).astype(jnp.float32)
    real_part = omegas[None, :] - freq_shift - level_row[:, None]
    imag_part = broadening * pole_sign[:, None]
    denominator = real_part * real_part + imag_part * imag_part
    return (real_part / denominator, -imag_part / denominator)


def spectrum(pair_real, pair_imag, green_real, green_imag):
    exact = lax.Precision.HIGHEST
    real_out = jnp.dot(pair_real, green_real, precision=exact) - jnp.dot(
        pair_imag, green_imag, precision=exact
    )
    imag_out = jnp.dot(pair_real, green_imag, precision=exact) + jnp.dot(
        pair_imag, green_real, precision=exact
    )
    return jnp.stack([real_out, imag_out])


def panel_product(density_all, screen):
    pair_rows = density_all.shape[1]
    panel_rows = screen.shape[1]
    product = lax.dot_general(
        density_all.reshape(2 * pair_rows, -1),
        screen.reshape(2 * panel_rows, -1),
        (((1,), (1,)), ((), ())),
        preferred_element_type=jnp.float32,
    )
    product = product.reshape(2, pair_rows, 2, panel_rows)
    return (product[0, :, 0] - product[1, :, 1], product[0, :, 1] + product[1, :, 0])


def body(densities, screened, energies, occupied, kmq, offsets, weights):
    qpoint = lax.axis_index("pb")
    my_freq = lax.axis_index("freq")
    my_panel = lax.axis_index("ga")
    count_pb = lax.axis_size("pb")
    count_freq = lax.axis_size("freq")
    screen = screened[0, 0]
    panel_width = screen.shape[1]
    local_block = densities[0]
    whole = lax.all_gather(local_block, ("freq", "ga"), axis=1, tiled=True)
    real_x, imag_x = panel_product(whole, screen)
    own_rows = lax.dynamic_slice_in_dim(whole, my_panel * panel_width, panel_width, 2)
    dense = own_rows.astype(jnp.float32)
    real_sum = jnp.sum(dense[0] * real_x + dense[1] * imag_x, axis=1)
    imag_sum = jnp.sum(dense[0] * imag_x - dense[1] * real_x, axis=1)
    pair_total = lax.psum(jnp.stack([real_sum, imag_sum]), "ga")
    weighted = (pair_total * weights[my_freq]).reshape(2, NS, NB)
    kpoint = kmq[qpoint]
    level_row = energies[kpoint]
    filled = occupied[kpoint]
    total_out = OUT_DEV * count_pb * count_freq
    index_grid = (jnp.arange(count_pb, dtype=jnp.int32)[:, None] * count_freq + my_freq) * OUT_DEV
    index_grid = (index_grid + jnp.arange(OUT_DEV, dtype=jnp.int32)[None, :]).reshape(-1)
    omegas = -2.0 + 4.0 * index_grid.astype(jnp.float32) / total_out
    summed = jnp.zeros((2, NS, count_pb * OUT_DEV), jnp.float32)
    passed = weighted
    for rotation in range(count_freq):
        anchor = (my_freq - rotation) % count_freq
        freq_shift = 4.0 * offsets[anchor].astype(jnp.float32) / total_out
        green_real, green_imag = green_parts(level_row, filled, freq_shift, omegas)
        summed = summed + spectrum(passed[0], passed[1], green_real, green_imag)
        if rotation + 1 < count_freq:
            passed = from_behind(passed, "freq", 1)
    local_part = lax.psum_scatter(summed, "pb", scatter_dimension=2, tiled=True)
    prefactor = 1.0 / (2.0 * math.pi * count_pb)
    return jnp.stack([-prefactor * local_part[1], prefactor * local_part[0]])


def solution(mesh):
    placed = (
        P("pb", None, ("freq", "ga"), None),
        P("pb", "freq", None, "ga", None),
        P(),
        P(),
        P(),
        P(),
        P(),
    )
    return jax.shard_map(
        body, mesh=mesh, in_specs=placed, out_specs=P(None, None, ("pb", "freq")), check_vma=False
    )
```

profile of v0, /device:TPU:0, one launch (start us, length us, event | category | flops | bytes accessed | tf_op | source)
XLA Modules:
  0.0 112.7 jit_solution(8596917107336101058)
XLA Ops:
  6.5 0.0 copy-start
  6.5 0.0 all-gather.3.cloned.1.call-start
  6.5 0.7 all-gather.3.cloned.1.call-update
  7.3 1.2 %dynamic_slice.30 = s32[1]{0:T(128)} dynamic-slice(s32[4]{0:T(128)} %param.11, s32[]{:T(128)S(6)} %select_n.62), dynamic_slice_sizes={1} | dynamic-slice | bytes 12 | tf_op jit(solution)/shard_map/dynamic_slice | solution.py:69
  9.9 1.5 %fusion.102 = (s32[1]{0:T(128)}, s32[1]{0:T(128)}, s32[1]{0:T(128)}, s32[1]{0:T(128)}) fusion(s32[4]{0:T(128)} %param.12, s32[]{:T(128)S(6)} %select_n.70, s32[]{:T(128)S(6)} %select_n.66, s32[]{:T(128)S(6)} %select_n.61, s32[]{:T(128)S(6)} %select_n.68), kind=kLoop, calls=%fused_computation.143 | loop fusion | bytes 48 | tf_op jit(solution)/shard_map/dynamic_slice | solution.py:80
  13.8 0.1 fusion.96
  13.9 0.1 reshape.335
  14.0 0.1 reshape.333
  14.1 0.1 reshape.331
  14.2 0.1 reshape.329
  14.2 1.3 %dynamic-slice.1 = u32[1]{0:T(128)} dynamic-slice(u32[32]{0:T(128)} %constant.95, u32[]{:T(128)S(6)} %add.222), dynamic_slice_sizes={1} | dynamic-slice | bytes 12
  16.1 1.3 %dynamic_slice.28 = f32[1]{0:T(128)} dynamic-slice(f32[4]{0:T(128)} %param.13, s32[]{:T(128)S(6)} %select_n.59), dynamic_slice_sizes={1} | dynamic-slice | bytes 12 | tf_op jit(solution)/shard_map/dynamic_slice | solution.py:68
  18.1 1.2 %dynamic_slice.32 = s32[1]{0:T(128)} dynamic-slice(s32[16]{0:T(128)} %param.10, s32[]{:T(128)S(6)} %select_n.63), dynamic_slice_sizes={1} | dynamic-slice | bytes 12 | tf_op jit(solution)/shard_map/dynamic_slice | solution.py:71
  19.3 0.0 copy-done
  19.3 0.7 fusion.100
  20.0 28.6 %all-gather.3.cloned.1.call-done = bf16[1,2,256,4096]{3,2,1,0:T(8,128)(2,1)} async-done(((bf16[1,2,32,4096]{3,2,1,0:T(8,128)(2,1)}), bf16[1,2,256,4096]{3,2,1,0:T(8,128)(2,1)}) %all-gather.3.cloned.1.call-update) | async-done | bytes 4194320 | tf_op jit(solution)/shard_map/all_gather | solution.py:61
  48.6 2.1 %dynamic-slice_convert_fusion = f32[1,2,256,2048]{3,2,1,0:T(8,128)S(1)} fusion(bf16[1,2,256,4096]{3,2,1,0:T(8,128)(2,1)} %all-gather.3.cloned.1.call-done, s32[]{:T(128)S(6)} %select_n.58), kind=kLoop, calls=%fused_computation.9 | loop fusion | flops 1048576 | bytes 6291460 | tf_op jit(solution)/shard_map/convert_element_type | solution.py:64
  50.7 22.8 %fusion = f32[2,256,2,2048]{3,1,2,0:T(8,128)S(1)} fusion(bf16[1,1,2,2048,4096]{4,3,2,1,0:T(8,128)(2,1)} %param.8, bf16[1,2,256,4096]{3,2,1,0:T(8,128)(2,1)} %all-gather.3.cloned.1.call-done), kind=kOutput, calls=%fused_computation | convolution fusion | flops 17179869184 | bytes 46137344 | tf_op jit(solution)/shard_map/dot_general | solution.py:42
  73.5 1.2 %add_reduce_fusion = (f32[256]{0:T(256)S(1)}, f32[256]{0:T(256)S(1)}) fusion(f32[1,2,256,2048]{3,2,1,0:T(8,128)S(1)} %dynamic-slice_convert_fusion, f32[2,256,2,2048]{3,1,2,0:T(8,128)S(1)} %fusion), kind=kLoop, calls=%fused_computation.11 | loop fusion | flops 5242368 | bytes 12584960 | tf_op jit(solution)/shard_map/reduce_sum | solution.py:65
  74.7 4.9 %psum.7 = f32[2,256]{1,0:T(2,128)S(1)} all-reduce(f32[2,256]{1,0:T(2,128)S(1)} %pad_maximum_fusion), channel_id=1, replica_groups=mesh['pb'=4,'freq'=4,'ga'=2] {'ga'}, use_global_device_ids=true, to_apply=%region_2.0 | all-reduce | flops 512 | bytes 4096 | tf_op jit(solution)/shard_map/psum | solution.py:67
  79.7 0.6 broadcast_multiply_fusion
  80.3 0.6 fusion.103
  80.9 0.3 convolution_bitcast_fusion.15
  81.2 0.3 convolution_bitcast_fusion.13
  81.5 0.3 fusion.13
  81.8 0.1 collective-permute-start
  81.9 0.3 fusion.14
  82.2 2.7 %collective-permute-done = f32[2,1,256]{2,0,1:T(2,128)S(1)} collective-permute-done((f32[2,1,256]{2,0,1:T(2,128)S(1)}, f32[2,1,256]{2,0,1:T(2,128)S(1)}, u32[]{:S(2)}, u32[]{:S(2)}) %collective-permute-start) | collective-permute-done | bytes 2080 | tf_op jit(solution)/shard_map/ppermute | solution.py:16
  84.9 0.3 convolution_bitcast_fusion.8
  85.2 0.3 convolution_bitcast_fusion.10
  85.5 0.1 collective-permute-start.1
  85.6 0.3 fusion.16
  85.9 0.3 fusion.15
  86.2 2.4 %collective-permute-done.1 = f32[2,1,256]{2,0,1:T(2,128)S(1)} collective-permute-done((f32[2,1,256]{2,0,1:T(2,128)S(1)}, f32[2,1,256]{2,0,1:T(2,128)S(1)}, u32[]{:S(2)}, u32[]{:S(2)}) %collective-permute-start.1) | collective-permute-done | bytes 2080 | tf_op jit(solution)/shard_map/ppermute | solution.py:16
  88.6 0.3 convolution_bitcast_fusion.4
  88.9 0.3 convolution_bitcast_fusion.6
  89.2 0.1 collective-permute-start.2
  89.3 0.3 fusion.18
  89.6 0.3 fusion.17
  89.9 2.4 %collective-permute-done.2 = f32[2,1,256]{2,0,1:T(2,128)S(1)} collective-permute-done((f32[2,1,256]{2,0,1:T(2,128)S(1)}, f32[2,1,256]{2,0,1:T(2,128)S(1)}, u32[]{:S(2)}, u32[]{:S(2)}) %collective-permute-start.2) | collective-permute-done | bytes 2080 | tf_op jit(solution)/shard_map/ppermute | solution.py:16
  92.3 0.3 convolution_bitcast_fusion
  92.6 0.3 convolution_bitcast_fusion.2
  92.9 0.3 fusion.20
  93.2 0.3 fusion.19
  93.5 11.7 %all-reduce = f32[2,1,16]{2,1,0:T(1,128)S(1)} all-reduce(f32[2,1,16]{2,1,0:T(1,128)S(1)} %fusion.99), channel_id=3, replica_groups=mesh['pb'=4,'freq'=4,'ga'=2] {'pb'}, use_global_device_ids=true, to_apply=%region_3.4.clone | all-reduce | flops 32 | bytes 256
  105.2 0.1 dynamic-slice_multiply_fusion.1
  105.3 0.6 pad_maximum_fusion.1
  (4 shorter events, 0.0 us)
Async XLA Ops:
  6.5 12.8 %copy-start = (f32[16,256]{1,0:T(8,128)S(1)}, f32[16,256]{1,0:T(8,128)}, u32[]{:S(2)}) copy-start(f32[16,256]{1,0:T(8,128)} %param.9) | copy-start | bytes 49156
  6.5 42.0 %all-gather.3.cloned.1.call-start = ((), (), s32[]{:S(2)}) async-start(), calls=%async_computation | async-start | bytes 4718592 | tf_op jit(solution)/shard_map/all_gather | solution.py:61
  81.8 3.1 %collective-permute-start = (f32[2,1,256]{2,0,1:T(2,128)S(1)}, f32[2,1,256]{2,0,1:T(2,128)S(1)}, u32[]{:S(2)}, u32[]{:S(2)}) collective-permute-start(f32[2,1,256]{2,0,1:T(2,128)S(1)} %fusion.103), channel_id=1, source_target_pairs={{6,0},{0,2},{2,4},{4,6},{7,1},{1,3},{3,5},{5,7},{14,8},{8,10},{10,... | collective-permute-start | bytes 6152 | tf_op jit(solution)/shard_map/ppermute | solution.py:16
  85.5 3.1 %collective-permute-start.1 = (f32[2,1,256]{2,0,1:T(2,128)S(1)}, f32[2,1,256]{2,0,1:T(2,128)S(1)}, u32[]{:S(2)}, u32[]{:S(2)}) collective-permute-start(f32[2,1,256]{2,0,1:T(2,128)S(1)} %collective-permute-done), channel_id=1, source_target_pairs={{6,0},{0,2},{2,4},{4,6},{7,1},{1,3},{3,5},{5,7},{14,8},{8,10},{10,... | collective-permute-start | bytes 6152 | tf_op jit(solution)/shard_map/ppermute | solution.py:16
  89.2 3.1 %collective-permute-start.2 = (f32[2,1,256]{2,0,1:T(2,128)S(1)}, f32[2,1,256]{2,0,1:T(2,128)S(1)}, u32[]{:S(2)}, u32[]{:S(2)}) collective-permute-start(f32[2,1,256]{2,0,1:T(2,128)S(1)} %collective-permute-done.1), channel_id=1, source_target_pairs={{6,0},{0,2},{2,4},{4,6},{7,1},{1,3},{3,5},{5,7},{14,8},{8,10},{10,... | collective-permute-start | bytes 6152 | tf_op jit(solution)/shard_map/ppermute | solution.py:16
Sparse Core Ops, SparseCore 0:
  9.2 39.2 all-gather.2
where the time goes:
time: 113 us
  waiting for transfers between devices  36.8 us (33%)
  matrix products  27.7 us (25%)
  between operations  18.7 us (17%)
  blocking collectives  16.6 us (15%)
  local copies, waits for them, and re-layouts  6.86 us (6%)
  other arithmetic  5.96 us (5%)
    all_gather x1, waiting for transfers between devices, body(): whole = lax.all_gather(local_block, ('freq', 'ga'), axis=1, tiled=True)  28.6 us
    dot_general x1, matrix products, panel_product(): lax.dot_general(density_all.reshape(2 * pair_rows, -1), screen.reshape(2...  22.8 us
    unnamed x1, blocking collectives  11.7 us
    ppermute x3, waiting for transfers between devices, from_behind(): return lax.ppermute(block, axis, route)  7.46 us
    psum x1, blocking collectives, body(): pair_total = lax.psum(jnp.stack([real_sum, imag_sum]), 'ga')  4.93 us
  transfers between devices with their start and end apart: 4, of which 4 were waited for; matrix products, arithmetic and copies ran while one was open for 8% of the time, Pallas kernels for 0%

commit v1 on v0

--- a/solution.py
+++ b/solution.py
@@ -1,3 +1,4 @@
+import functools
 import math
 import jax
 import jax.numpy as jnp
@@ -8,6 +9,13 @@
 NS = 1
 OUT_DEV = 4
 broadening = 0.15
+
+
+def spread_trails_in(block_in, axis_key):
+    return jnp.concatenate(lax.all_gather(block_in, axis_key), axis=1)
+
+
+find_the_unit = functools.partial(spread_trails_in, axis_key=("freq", "ga"))
 
 
 def from_behind(block, axis, distance):
@@ -58,7 +66,7 @@
     screen = screened[0, 0]
     panel_width = screen.shape[1]
     local_block = densities[0]
-    whole = lax.all_gather(local_block, ("freq", "ga"), axis=1, tiled=True)
+    whole = find_the_unit(local_block)
     real_x, imag_x = panel_product(whole, screen)
     own_rows = lax.dynamic_slice_in_dim(whole, my_panel * panel_width, panel_width, 2)
     dense = own_rows.astype(jnp.float32)

time: 113 us -> 118 us (1.044)
  local copies, waits for them, and re-layouts: 6.86 us -> 9.51 us
  other arithmetic: 5.96 us -> 7.79 us
    reduce_sum x1, other arithmetic: 1.22 us -> 4.6 us  [body(): real_sum = jnp.sum(dense[0] * real_x + dense[1] * imag_x, axis=1)]
    reshape x0 -> x1, local copies, waits for them, and re-layouts: none -> 2.67 us  [spread_trails_in(): return jnp.concatenate(lax.all_gather(block_in, axis_key), axis=1)]
    convert_element_type x1, other arithmetic: 2.1 us -> 0.52 us  [body(): dense = own_rows.astype(jnp.float32)]
where the time goes in v1:
time: 118 us; the launch traced here: 117 us
  waiting for transfers between devices  36.8 us (31%)
  matrix products  27.8 us (24%)
  between operations  18.7 us (16%)
  blocking collectives  16.6 us (14%)
  local copies, waits for them, and re-layouts  9.51 us (8%)
  other arithmetic  7.79 us (7%)
    all_gather x1, waiting for transfers between devices, spread_trails_in(): return jnp.concatenate(lax.all_gather(block_in, axis_key), axis=1)  28.6 us
    dot_general x1, matrix products, panel_product(): lax.dot_general(density_all.reshape(2 * pair_rows, -1), screen.reshape(2...  23 us
    unnamed x1, blocking collectives  11.7 us
    ppermute x3, waiting for transfers between devices, from_behind(): return lax.ppermute(block, axis, route)  7.46 us
    psum x1, blocking collectives, body(): pair_total = lax.psum(jnp.stack([real_sum, imag_sum]), 'ga')  4.93 us
    reduce_sum x1, other arithmetic, body(): real_sum = jnp.sum(dense[0] * real_x + dense[1] * imag_x, axis=1)  4.6 us
    reshape x1, local copies, waits for them, and re-layouts, spread_trails_in(): return jnp.concatenate(lax.all_gather(block_in, axis_key), axis=1)  2.67 us
  transfers between devices with their start and end apart: 4, of which 4 were waited for; matrix products, arithmetic and copies ran while one was open for 8% of the time, Pallas kernels for 0%

profile of v1, /device:TPU:0, one launch (start us, length us, event | category | flops | bytes accessed | tf_op | source)
XLA Modules:
  0.0 117.4 jit_solution(7099264643580606152)
XLA Ops:
  6.5 0.0 copy-start
  6.5 0.0 all-gather.2.cloned.1.call-start
  6.5 0.7 all-gather.2.cloned.1.call-update
  7.3 1.2 %dynamic_slice.30 = s32[1]{0:T(128)} dynamic-slice(s32[4]{0:T(128)} %param.11, s32[]{:T(128)S(6)} %select_n.62), dynamic_slice_sizes={1} | dynamic-slice | bytes 12 | tf_op jit(solution)/shard_map/dynamic_slice | solution.py:77
  9.9 1.5 %fusion.101 = (s32[1]{0:T(128)}, s32[1]{0:T(128)}, s32[1]{0:T(128)}, s32[1]{0:T(128)}) fusion(s32[4]{0:T(128)} %param.12, s32[]{:T(128)S(6)} %select_n.70, s32[]{:T(128)S(6)} %select_n.66, s32[]{:T(128)S(6)} %select_n.61, s32[]{:T(128)S(6)} %select_n.68), kind=kLoop, calls=%fused_computation.142 | loop fusion | bytes 48 | tf_op jit(solution)/shard_map/dynamic_slice | solution.py:88
  13.8 0.1 fusion.95
  13.9 0.1 reshape.342
  14.0 0.1 reshape.340
  14.1 0.1 reshape.338
  14.2 0.1 reshape.336
  14.2 1.3 %dynamic-slice = u32[1]{0:T(128)} dynamic-slice(u32[32]{0:T(128)} %constant.94, u32[]{:T(128)S(6)} %add.222), dynamic_slice_sizes={1} | dynamic-slice | bytes 12
  16.1 1.3 %dynamic_slice.28 = f32[1]{0:T(128)} dynamic-slice(f32[4]{0:T(128)} %param.13, s32[]{:T(128)S(6)} %select_n.59), dynamic_slice_sizes={1} | dynamic-slice | bytes 12 | tf_op jit(solution)/shard_map/dynamic_slice | solution.py:76
  18.0 1.2 %dynamic_slice.32 = s32[1]{0:T(128)} dynamic-slice(s32[16]{0:T(128)} %param.10, s32[]{:T(128)S(6)} %select_n.63), dynamic_slice_sizes={1} | dynamic-slice | bytes 12 | tf_op jit(solution)/shard_map/dynamic_slice | solution.py:79
  19.3 0.0 copy-done
  19.3 0.7 fusion.99
  20.0 28.6 %all-gather.2.cloned.1.call-done = bf16[8,2,32,4096]{3,2,1,0:T(8,128)(2,1)} async-done(((bf16[1,2,32,4096]{3,2,1,0:T(8,128)(2,1)}), bf16[8,2,32,4096]{3,2,1,0:T(8,128)(2,1)}) %all-gather.2.cloned.1.call-update) | async-done | bytes 4194320 | tf_op jit(solution)/shard_map/all_gather | solution.py:15
  48.6 2.7 %copy.9 = bf16[2,8,32,4096]{3,2,1,0:T(8,128)(2,1)S(1)} copy(bf16[2,8,32,4096]{3,2,0,1:T(8,128)(2,1)} %bitcast.187) | data formatting | bytes 8388608 | tf_op jit(solution)/shard_map/reshape | solution.py:15
  51.2 0.5 dynamic-slice_convert_fusion
  51.8 23.0 %fusion = f32[2,256,2,2048]{3,1,2,0:T(8,128)} fusion(bf16[2,256,4096,1]{2,1,3,0:T(8,128)(2,1)S(1)} %bitcast.186, bf16[1,1,2,2048,4096]{4,3,2,1,0:T(8,128)(2,1)} %param.8), kind=kOutput, calls=%fused_computation | convolution fusion | flops 17179869184 | bytes 46137344 | tf_op jit(solution)/shard_map/dot_general | solution.py:50
  74.7 4.6 %add_reduce_fusion = (f32[256]{0:T(256)S(1)}, f32[256]{0:T(256)S(1)}) fusion(f32[2,256,2048]{2,1,0:T(8,128)S(1)} %dynamic-slice_convert_fusion, f32[2,256,2,2048]{3,1,2,0:T(8,128)} %fusion), kind=kLoop, calls=%fused_computation.9 | loop fusion | flops 5242368 | bytes 12584960 | tf_op jit(solution)/shard_map/reduce_sum | solution.py:73
  79.4 4.9 %psum.7 = f32[2,256]{1,0:T(2,128)S(1)} all-reduce(f32[2,256]{1,0:T(2,128)S(1)} %pad_maximum_fusion), channel_id=1, replica_groups=mesh['pb'=4,'freq'=4,'ga'=2] {'ga'}, use_global_device_ids=true, to_apply=%region_2.0 | all-reduce | flops 512 | bytes 4096 | tf_op jit(solution)/shard_map/psum | solution.py:75
  84.3 0.6 broadcast_multiply_fusion
  84.9 0.6 fusion.103
  85.6 0.3 convolution_bitcast_fusion.15
  85.9 0.3 convolution_bitcast_fusion.13
  86.2 0.3 fusion.12
  86.5 0.1 collective-permute-start
  86.6 0.3 fusion.13
  86.9 2.7 %collective-permute-done = f32[2,1,256]{2,0,1:T(2,128)S(1)} collective-permute-done((f32[2,1,256]{2,0,1:T(2,128)S(1)}, f32[2,1,256]{2,0,1:T(2,128)S(1)}, u32[]{:S(2)}, u32[]{:S(2)}) %collective-permute-start) | collective-permute-done | bytes 2080 | tf_op jit(solution)/shard_map/ppermute | solution.py:24
  89.6 0.3 convolution_bitcast_fusion.8
  89.9 0.3 convolution_bitcast_fusion.10
  90.2 0.1 collective-permute-start.1
  90.3 0.3 fusion.15
  90.6 0.3 fusion.14
  90.9 2.4 %collective-permute-done.1 = f32[2,1,256]{2,0,1:T(2,128)S(1)} collective-permute-done((f32[2,1,256]{2,0,1:T(2,128)S(1)}, f32[2,1,256]{2,0,1:T(2,128)S(1)}, u32[]{:S(2)}, u32[]{:S(2)}) %collective-permute-start.1) | collective-permute-done | bytes 2080 | tf_op jit(solution)/shard_map/ppermute | solution.py:24
  93.2 0.3 convolution_bitcast_fusion.4
  93.5 0.3 convolution_bitcast_fusion.6
  93.9 0.1 collective-permute-start.2
  93.9 0.3 fusion.17
  94.2 0.3 fusion.16
  94.5 2.4 %collective-permute-done.2 = f32[2,1,256]{2,0,1:T(2,128)S(1)} collective-permute-done((f32[2,1,256]{2,0,1:T(2,128)S(1)}, f32[2,1,256]{2,0,1:T(2,128)S(1)}, u32[]{:S(2)}, u32[]{:S(2)}) %collective-permute-start.2) | collective-permute-done | bytes 2080 | tf_op jit(solution)/shard_map/ppermute | solution.py:24
  96.9 0.3 convolution_bitcast_fusion
  97.2 0.3 convolution_bitcast_fusion.2
  97.5 0.3 fusion.19
  97.9 0.3 fusion.18
  98.2 11.7 %all-reduce = f32[2,1,16]{2,1,0:T(1,128)S(1)} all-reduce(f32[2,1,16]{2,1,0:T(1,128)S(1)} %fusion.98), channel_id=2, replica_groups=mesh['pb'=4,'freq'=4,'ga'=2] {'pb'}, use_global_device_ids=true, to_apply=%region_3.4.clone | all-reduce | flops 32 | bytes 256
  109.9 0.1 dynamic-slice_multiply_fusion.1
  110.0 0.6 pad_maximum_fusion.1
  (4 shorter events, 0.0 us)
Async XLA Ops:
  6.5 12.8 %copy-start = (f32[16,256]{1,0:T(8,128)S(1)}, f32[16,256]{1,0:T(8,128)}, u32[]{:S(2)}) copy-start(f32[16,256]{1,0:T(8,128)} %param.9) | copy-start | bytes 49156
  6.5 42.0 %all-gather.2.cloned.1.call-start = ((), (), s32[]{:S(2)}) async-start(), calls=%async_computation | async-start | bytes 4718592 | tf_op jit(solution)/shard_map/all_gather | solution.py:15
  86.5 3.1 %collective-permute-start = (f32[2,1,256]{2,0,1:T(2,128)S(1)}, f32[2,1,256]{2,0,1:T(2,128)S(1)}, u32[]{:S(2)}, u32[]{:S(2)}) collective-permute-start(f32[2,1,256]{2,0,1:T(2,128)S(1)} %fusion.103), channel_id=1, source_target_pairs={{6,0},{0,2},{2,4},{4,6},{7,1},{1,3},{3,5},{5,7},{14,8},{8,10},{10,... | collective-permute-start | bytes 6152 | tf_op jit(solution)/shard_map/ppermute | solution.py:24
  90.2 3.1 %collective-permute-start.1 = (f32[2,1,256]{2,0,1:T(2,128)S(1)}, f32[2,1,256]{2,0,1:T(2,128)S(1)}, u32[]{:S(2)}, u32[]{:S(2)}) collective-permute-start(f32[2,1,256]{2,0,1:T(2,128)S(1)} %collective-permute-done), channel_id=1, source_target_pairs={{6,0},{0,2},{2,4},{4,6},{7,1},{1,3},{3,5},{5,7},{14,8},{8,10},{10,... | collective-permute-start | bytes 6152 | tf_op jit(solution)/shard_map/ppermute | solution.py:24
  93.9 3.1 %collective-permute-start.2 = (f32[2,1,256]{2,0,1:T(2,128)S(1)}, f32[2,1,256]{2,0,1:T(2,128)S(1)}, u32[]{:S(2)}, u32[]{:S(2)}) collective-permute-start(f32[2,1,256]{2,0,1:T(2,128)S(1)} %collective-permute-done.1), channel_id=1, source_target_pairs={{6,0},{0,2},{2,4},{4,6},{7,1},{1,3},{3,5},{5,7},{14,8},{8,10},{10,... | collective-permute-start | bytes 6152 | tf_op jit(solution)/shard_map/ppermute | solution.py:24
Sparse Core Ops, SparseCore 0:
  9.2 39.2 all-gather.1
